TPU v7x, 32 devices: a whole 2x2x4 slice. The times are simulated.
32 devices in a mesh: bank: 4 (over y, x), zero: 8 (over z, core).
Axes of the slice: x: 2, y: 2, z: 4, core: 2. Of those that a mesh axis runs over, the one named last changes fastest.
Arguments:
- train_gate: float32 [64, 2048, 1024], P('bank', 'zero'), may hold values from -0.1875 to 0.1875
- train_up: float32 [64, 2048, 1024], P('bank', 'zero'), may hold values from -0.1875 to 0.1875
- train_down: float32 [64, 1024, 2048], P('bank', None, 'zero'), may hold values from -0.25 to 0.25
- router_weight: float32 [2048, 64], P('zero', 'bank'), may hold values from -0.125 to 0.125
- router_gain: float32 [2048], P('zero'), may hold values from 0.25 to 1.75
Outputs:
- ready_gate: bfloat16 [64, 2048, 1024], P('bank', None, 'zero')
- ready_up: bfloat16 [64, 2048, 1024], P('bank', None, 'zero')
- ready_down: bfloat16 [64, 1024, 2048], P('bank', 'zero')
- scale_gate: float32 [64, 1024], P('bank', 'zero')
- scale_up: float32 [64, 1024], P('bank', 'zero')
- scale_down: float32 [64, 1024], P('bank', 'zero')
- serve_router: bfloat16 [2048, 64], replicated
All inputs are finite; a program needn't handle non-finite values.
Results may differ from a plain program's by a relative error of at most 0.001.
Values may be sent and summed in bfloat16 or wider, within the bound.
A program may use at most 192 MiB of HBM per device.

v0:
```python
import jax
import jax.numpy as jnp
from jax import lax
from jax.sharding import PartitionSpec as P


def on_device(train_gate, train_up, train_down, router_weight, router_gain):
    total_gate, total_up, total_down = lax.psum(
        (
            jnp.sum(train_gate * train_gate, axis=1),
            jnp.sum(train_up * train_up, axis=1),
            jnp.sum(train_down * train_down, axis=2),
        ),
        "zero",
    )
    scale_gate = jnp.sqrt(total_gate)
    scale_up = jnp.sqrt(total_up)
    scale_down = jnp.sqrt(total_down)
    narrow_gate, narrow_up, narrow_down = (
        (train_gate / jnp.expand_dims(scale_gate, 1)).astype(jnp.bfloat16),
        (train_up / jnp.expand_dims(scale_up, 1)).astype(jnp.bfloat16),
        (train_down / jnp.expand_dims(scale_down, 2)).astype(jnp.bfloat16),
    )
    ready_gate, ready_up = (
        lax.all_to_all(narrow_gate, "zero", split_axis=2, concat_axis=1, tiled=True),
        lax.all_to_all(narrow_up, "zero", split_axis=2, concat_axis=1, tiled=True),
    )
    ready_down = lax.all_to_all(narrow_down, "zero", split_axis=1, concat_axis=2, tiled=True)
    scale_gate = lax.dynamic_slice_in_dim(
        scale_gate, lax.axis_index("zero") * ready_gate.shape[2], ready_gate.shape[2], axis=1
    )
    scale_up = lax.dynamic_slice_in_dim(
        scale_up, lax.axis_index("zero") * ready_up.shape[2], ready_up.shape[2], axis=1
    )
    scale_down = lax.dynamic_slice_in_dim(
        scale_down, lax.axis_index("zero") * ready_down.shape[1], ready_down.shape[1], axis=1
    )
    part_router = (router_weight * router_gain[:, None]).astype(jnp.bfloat16)
    row_router = lax.all_gather(part_router, "zero", axis=0, tiled=True)
    serve_router = lax.all_gather(row_router, "bank", axis=1, tiled=True)
    return (ready_gate, ready_up, ready_down, scale_gate, scale_up, scale_down, serve_router)


def solution(mesh):
    return jax.shard_map(
        on_device,
        mesh=mesh,
        in_specs=(
            P("bank", "zero", None),
            P("bank", "zero", None),
            P("bank", None, "zero"),
            P("zero", "bank"),
            P("zero"),
        ),
        out_specs=(
            P("bank", None, "zero"),
            P("bank", None, "zero"),
            P("bank", "zero", None),
            P("bank", "zero"),
            P("bank", "zero"),
            P("bank", "zero"),
            P(),
        ),
        check_vma=False,
    )
```

profile of v0, /device:TPU:0, one launch (start us, length us, event | category | flops | bytes accessed | tf_op | source)
XLA Modules:
  0.0 737.8 jit_solution(13230997140834230480)
XLA Ops:
  7.2 0.0 all-reduce.3.cloned.1.call-start
  7.2 8.6 %multiply_reduce_fusion = f32[16,1024]{1,0:T(8,128)} fusion(f32[16,1024,256]{2,1,0:T(8,128)} %param.7), kind=kLoop, calls=%fused_computation.2 | loop fusion | flops 8372224 | bytes 16842752 | tf_op jit(solution)/shard_map/reduce_sum | solution.py:12
  15.8 12.6 %multiply_reduce_fusion.1 = (f32[16,1024]{1,0:T(8,128)}, f32[16,1024]{1,0:T(8,128)}) fusion(f32[16,256,1024]{2,1,0:T(8,128)} %param.6, f32[16,256,1024]{2,1,0:T(8,128)} %param.5), kind=kLoop, calls=%fused_computation.4 | loop fusion | flops 16744448 | bytes 33685504 | tf_op jit(solution)/shard_map/reduce_sum | solution.py:11
  28.4 0.0 all-reduce.3.cloned.1.call-update
  28.4 17.6 %copy.19 = f32[16,256,1024]{1,0,2:T(8,128)} copy(f32[16,256,1024]{2,1,0:T(8,128)} %param.6) | data formatting | bytes 33554432 | tf_op args[1]
  46.1 40.7 %all-reduce.3.cloned.1.call-done = (f32[16,1024]{1,0:T(8,128)}, f32[16,1024]{1,0:T(8,128)}, f32[16,1024]{1,0:T(8,128)}) async-done(((f32[16,1024]{1,0:T(8,128)}, f32[16,1024]{1,0:T(8,128)}, f32[16,1024]{1,0:T(8,128)}), (f32[16,1024]{1,0:T(8,128)}, f32[16,1024]{1,0:T(8,128)}, f32[16,1024]{1,0:T(8,128)})) %all-reduce.3.cloned.1.call-update) | async-done | bytes 196624 | tf_op jit(solution)/shard_map/psum | solution.py:8
  86.8 0.9 sqrt.10
  87.6 0.2 copy.18
  87.8 9.6 %divide_convert_fusion = bf16[16,256,1024]{1,0,2:T(8,128)(2,1)} fusion(f32[16,256,1024]{1,0,2:T(8,128)} %copy.19, f32[16,1024]{0,1:T(8,128)S(1)} %copy.18), kind=kLoop, calls=%fused_computation.3 | loop fusion | flops 8388608 | bytes 25231360 | tf_op jit(solution)/shard_map/convert_element_type | solution.py:21
  97.5 4.9 all-to-all-start.1
  102.4 0.0 copy-start.1
  102.4 17.6 %copy.16 = f32[16,256,1024]{1,0,2:T(8,128)} copy(f32[16,256,1024]{2,1,0:T(8,128)} %param.5) | data formatting | bytes 33554432 | tf_op args[0]
  120.1 0.0 copy-done.1
  120.1 0.2 copy.15
  120.3 0.0 copy-start
  120.3 9.7 %divide_convert_fusion.1 = bf16[16,256,1024]{1,0,2:T(8,128)(2,1)} fusion(f32[16,256,1024]{1,0,2:T(8,128)} %copy.16, f32[16,1024]{0,1:T(8,128)S(1)} %copy.15), kind=kLoop, calls=%fused_computation.5 | loop fusion | flops 8388608 | bytes 25231360 | tf_op jit(solution)/shard_map/convert_element_type | solution.py:20
  130.0 156.3 %all-to-all-done.1 = bf16[16,256,1024]{1,0,2:T(8,128)(2,1)} async-done(((bf16[16,256,1024]{1,0,2:T(8,128)(2,1)}), bf16[16,256,1024]{1,0,2:T(8,128)(2,1)}, u32[]{:S(2)}, u32[]{:S(2)}) %all-to-all-start.1) | async-done | bytes 8388640 | tf_op jit(solution)/shard_map/all_to_all | solution.py:26
  286.3 4.9 all-to-all-start
  291.2 0.0 copy-done
  291.3 0.2 copy.21
  291.5 0.0 copy-start.2
  291.5 0.0 copy-start.3
  291.5 16.6 %fusion = bf16[16,1024,256]{2,0,1:T(8,128)(2,1)} fusion(f32[16,1024,256]{2,1,0:T(8,128)} %param.7, f32[16,1024]{0,1:T(8,128)S(1)} %copy.21), kind=kLoop, calls=%fused_computation.1 | loop fusion | flops 8388608 | bytes 25231360 | tf_op jit(solution)/shard_map/convert_element_type | solution.py:22
  308.1 167.0 %all-to-all-done = bf16[16,256,1024]{1,0,2:T(8,128)(2,1)} async-done(((bf16[16,256,1024]{1,0,2:T(8,128)(2,1)}), bf16[16,256,1024]{1,0,2:T(8,128)(2,1)}, u32[]{:S(2)}, u32[]{:S(2)}) %all-to-all-start) | async-done | bytes 8388640 | tf_op jit(solution)/shard_map/all_to_all | solution.py:25
  475.1 5.0 all-to-all-start.2
  480.1 0.0 copy-done.2
  480.1 0.0 copy-done.3
  480.2 189.9 %all_gather.6 = bf16[2048,16]{0,1:T(8,128)(2,1)S(1)} all-gather(bf16[256,16]{0,1:T(8,128)(2,1)S(1)} %multiply_convert_fusion), channel_id=1, replica_groups=mesh['bank'=4,'zero'=8] {'zero'}, dimensions={0}, use_global_device_ids=true | all-gather | bytes 73728 | tf_op jit(solution)/shard_map/all_gather | solution.py:39
  670.0 9.1 %all_gather.7 = bf16[2048,64]{0,1:T(8,128)(2,1)S(1)} all-gather(bf16[2048,16]{0,1:T(8,128)(2,1)S(1)} %all_gather.6), channel_id=1, replica_groups=mesh['bank'=4,'zero'=8] {'bank'}, dimensions={1}, use_global_device_ids=true | all-gather | bytes 327680 | tf_op jit(solution)/shard_map/all_gather | solution.py:40
  679.1 0.6 constant_dynamic-slice_fusion
  679.7 0.6 constant_dynamic-slice_fusion.1
  680.3 0.6 constant_dynamic-slice_fusion.2
  680.9 12.3 %copy.20 = bf16[16,8,256,128]{3,2,1,0:T(8,128)(2,1)} copy(bf16[16,8,256,128]{2,0,3,1:T(8,128)(2,1)} %bitcast.4) | data formatting | bytes 16777216 | tf_op jit(solution)/shard_map/all_to_all | solution.py:26
  693.2 12.3 %copy.17 = bf16[16,8,256,128]{3,2,1,0:T(8,128)(2,1)} copy(bf16[16,8,256,128]{2,0,3,1:T(8,128)(2,1)} %bitcast.1) | data formatting | bytes 16777216 | tf_op jit(solution)/shard_map/all_to_all | solution.py:25
  705.5 0.0 all-to-all-done.2
  705.5 11.4 %copy.23 = bf16[16,128,8,256]{3,2,1,0:T(8,128)(2,1)} copy(bf16[16,128,8,256]{3,0,1,2:T(8,128)(2,1)} %bitcast.7) | data formatting | bytes 16777216 | tf_op jit(solution)/shard_map/all_to_all | solution.py:28
  716.9 13.4 %all_to_all.50 = bf16[16,128,2048]{2,1,0:T(8,128)(2,1)} reshape(bf16[16,128,8,256]{3,2,1,0:T(8,128)(2,1)} %copy.23) | data formatting | bytes 16777216 | tf_op jit(solution)/shard_map/all_to_all | solution.py:28
  730.3 0.7 copy.31
  (3 shorter events, 0.0 us)
Async XLA Ops:
  7.2 79.6 %all-reduce.3.cloned.1.call-start = ((), (), s32[]{:S(2)}) async-start(), calls=%async_computation.3 | async-start | bytes 393216 | tf_op jit(solution)/shard_map/psum | solution.py:8
  97.5 188.8 %all-to-all-start.1 = ((bf16[16,256,1024]{1,0,2:T(8,128)(2,1)}), bf16[16,256,1024]{1,0,2:T(8,128)(2,1)}, u32[]{:S(2)}, u32[]{:S(2)}) async-start(bf16[16,256,1024]{1,0,2:T(8,128)(2,1)} %divide_convert_fusion), calls=%async_computation.1 | async-start | bytes 16777216 | tf_op jit(solution)/shard_map/all_to_all | solution.py:26
  102.4 17.6 %copy-start.1 = (f32[16,1024]{1,0:T(8,128)S(1)}, f32[16,1024]{1,0:T(8,128)}, u32[]{:S(2)}) copy-start(f32[16,1024]{1,0:T(8,128)} %get-tuple-element.7) | copy-start | bytes 196612
  120.3 170.9 %copy-start = (f32[16,1024]{1,0:T(8,128)S(1)}, f32[16,1024]{1,0:T(8,128)}, u32[]{:S(2)}) copy-start(f32[16,1024]{1,0:T(8,128)} %get-tuple-element.9) | copy-start | bytes 196612
  286.3 188.8 %all-to-all-start = ((bf16[16,256,1024]{1,0,2:T(8,128)(2,1)}), bf16[16,256,1024]{1,0,2:T(8,128)(2,1)}, u32[]{:S(2)}, u32[]{:S(2)}) async-start(bf16[16,256,1024]{1,0,2:T(8,128)(2,1)} %divide_convert_fusion.1), calls=%async_computation | async-start | bytes 16777216 | tf_op jit(solution)/shard_map/all_to_all | solution.py:25
  291.5 188.6 %copy-start.2 = (f32[256,16]{0,1:T(8,128)S(1)}, f32[256,16]{0,1:T(8,128)}, u32[]{:S(2)}) copy-start(f32[256,16]{0,1:T(8,128)} %param.8) | copy-start | bytes 49156
  291.5 188.6 %copy-start.3 = (f32[256]{0:T(256)S(1)}, f32[256]{0:T(256)}, u32[]{:S(2)}) copy-start(f32[256]{0:T(256)} %param.9) | copy-start | bytes 3076
  475.1 230.4 %all-to-all-start.2 = ((bf16[16,1024,256]{2,0,1:T(8,128)(2,1)}), bf16[16,1024,256]{2,0,1:T(8,128)(2,1)}, u32[]{:S(2)}, u32[]{:S(2)}) async-start(bf16[16,1024,256]{2,0,1:T(8,128)(2,1)} %fusion), calls=%async_computation.2 | async-start | bytes 16777216 | tf_op jit(solution)/shard_map/all_to_all | solution.py:28
Sparse Core Ops, SparseCore 0:
  28.6 58.1 all-reduce.2
where the time goes:
time: 740 us; the launch traced here: 738 us
  waiting for transfers between devices  364 us (49%)
  blocking collectives  199 us (27%)
  local copies, waits for them, and re-layouts  88.6 us (12%)
  other arithmetic  57.2 us (8%)
  starting transfers between devices  14.9 us (2%)
  between operations  14.2 us (2%)
    all_gather x1, blocking collectives, on_device(): row_router = lax.all_gather(part_router, 'zero', axis=0, tiled=True)  190 us
    all_to_all x1, waiting for transfers between devices, on_device(): lax.all_to_all(narrow_gate, 'zero', split_axis=2, concat_axis=1, tiled=True)  167 us
    all_to_all x1, waiting for transfers between devices, on_device(): lax.all_to_all(narrow_up, 'zero', split_axis=2, concat_axis=1, tiled=True)  156 us
    psum x1, waiting for transfers between devices, on_device(): lax.psum((jnp.sum(train_gate * train_gate, axis=1), jnp.sum(train_up * tr...  40.7 us
    unnamed x11, local copies, waits for them, and re-layouts  36 us
    all_to_all x2, local copies, waits for them, and re-layouts, on_device(): lax.all_to_all(narrow_down, 'zero', split_axis=1, concat_axis=2, tiled=True)  24.8 us
    convert_element_type x1, other arithmetic, on_device(): (train_down / jnp.expand_dims(scale_down, 2)).astype(jnp.bfloat16)  16.6 us
  transfers between devices with their start and end apart: 4, of which 3 were waited for; matrix products, arithmetic and copies ran while one was open for 12% of the time, Pallas kernels for 0%

commit v1 on v0

--- a/solution.py
+++ b/solution.py
@@ -36,7 +36,9 @@
         scale_down, lax.axis_index("zero") * ready_down.shape[1], ready_down.shape[1], axis=1
     )
     part_router = (router_weight * router_gain[:, None]).astype(jnp.bfloat16)
-    row_router = lax.all_gather(part_router, "zero", axis=0, tiled=True)
+    row_router = jnp.concatenate(
+        lax.all_to_all(jnp.stack([part_router] * lax.axis_size("zero")), "zero", 0, 0), axis=0
+    )
     serve_router = lax.all_gather(row_router, "bank", axis=1, tiled=True)
     return (ready_gate, ready_up, ready_down, scale_gate, scale_up, scale_down, serve_router)
 

time: 740 us -> 698 us (0.943)
  blocking collectives: 199 us -> 9.11 us
  waiting for transfers between devices: 364 us -> 505 us
    all_gather x1 -> x0, blocking collectives: 190 us -> none  [on_device(): row_router = lax.all_gather(part_router, 'zero', axis=0, tiled=True)]
    all_to_all x1, waiting for transfers between devices: 0.01 us -> 148 us  [on_device(): lax.all_to_all(narrow_down, 'zero', split_axis=1, concat_axis=2, tiled=True)]
  transfers between devices with their start and end apart: 4 -> 5, of which waited for: 3 -> 4; matrix products, arithmetic and copies ran while one was open for 12% -> 14% of each run, Pallas kernels for 0% -> 0%
where the time goes in v1:
time: 698 us; the launch traced here: 696 us
  waiting for transfers between devices  505 us (72%)
  local copies, waits for them, and re-layouts  89.2 us (13%)
  other arithmetic  57.2 us (8%)
  starting transfers between devices  21.3 us (3%)
  between operations  14.2 us (2%)
  blocking collectives  9.11 us (1%)
    all_to_all x1, waiting for transfers between devices, on_device(): lax.all_to_all(narrow_gate, 'zero', split_axis=2, concat_axis=1, tiled=True)  167 us
    all_to_all x1, waiting for transfers between devices, on_device(): lax.all_to_all(narrow_up, 'zero', split_axis=2, concat_axis=1, tiled=True)  156 us
    all_to_all x1, waiting for transfers between devices, on_device(): lax.all_to_all(narrow_down, 'zero', split_axis=1, concat_axis=2, tiled=True)  148 us
    unnamed x11, local copies, waits for them, and re-layouts  36 us
    psum x1, waiting for transfers between devices, on_device(): lax.psum((jnp.sum(train_gate * train_gate, axis=1), jnp.sum(train_up * tr...  33.8 us
    all_to_all x2, local copies, waits for them, and re-layouts, on_device(): lax.all_to_all(narrow_down, 'zero', split_axis=1, concat_axis=2, tiled=True)  24.8 us
    convert_element_type x1, other arithmetic, on_device(): (train_down / jnp.expand_dims(scale_down, 2)).astype(jnp.bfloat16)  16.6 us
  transfers between devices with their start and end apart: 5, of which 4 were waited for; matrix products, arithmetic and copies ran while one was open for 14% of the time, Pallas kernels for 0%

profile of v1, /device:TPU:0, one launch (start us, length us, event | category | flops | bytes accessed | tf_op | source)
XLA Modules:
  0.0 696.5 jit_solution(6480954519635393990)
XLA Ops:
  7.2 0.0 all-reduce.3.cloned.1.call-start
  7.2 8.6 %multiply_reduce_fusion = f32[16,1024]{1,0:T(8,128)} fusion(f32[16,1024,256]{2,1,0:T(8,128)} %param.7), kind=kLoop, calls=%fused_computation.2 | loop fusion | flops 8372224 | bytes 16842752 | tf_op jit(solution)/shard_map/reduce_sum | solution.py:12
  15.8 0.0 copy-start.2
  15.8 0.0 copy-start.3
  15.9 12.6 %multiply_reduce_fusion.1 = (f32[16,1024]{1,0:T(8,128)}, f32[16,1024]{1,0:T(8,128)}) fusion(f32[16,256,1024]{2,1,0:T(8,128)} %param.6, f32[16,256,1024]{2,1,0:T(8,128)} %param.5), kind=kLoop, calls=%fused_computation.4 | loop fusion | flops 16744448 | bytes 33685504 | tf_op jit(solution)/shard_map/reduce_sum | solution.py:11
  28.4 0.0 all-reduce.3.cloned.1.call-update
  28.5 0.0 copy-done.2
  28.5 0.0 copy-done.3
  28.5 0.6 stack.2
  29.1 6.4 all-to-all-start.3
  35.5 17.6 %copy.28 = f32[16,256,1024]{1,0,2:T(8,128)} copy(f32[16,256,1024]{2,1,0:T(8,128)} %param.6) | data formatting | bytes 33554432 | tf_op args[1]
  53.1 33.8 %all-reduce.3.cloned.1.call-done = (f32[16,1024]{1,0:T(8,128)}, f32[16,1024]{1,0:T(8,128)}, f32[16,1024]{1,0:T(8,128)}) async-done(((f32[16,1024]{1,0:T(8,128)}, f32[16,1024]{1,0:T(8,128)}, f32[16,1024]{1,0:T(8,128)}), (f32[16,1024]{1,0:T(8,128)}, f32[16,1024]{1,0:T(8,128)}, f32[16,1024]{1,0:T(8,128)})) %all-reduce.3.cloned.1.call-update) | async-done | bytes 196624 | tf_op jit(solution)/shard_map/psum | solution.py:8
  86.9 0.9 sqrt.10
  87.8 0.2 copy.27
  88.0 9.6 %divide_convert_fusion = bf16[16,256,1024]{1,0,2:T(8,128)(2,1)} fusion(f32[16,256,1024]{1,0,2:T(8,128)} %copy.28, f32[16,1024]{0,1:T(8,128)S(1)} %copy.27), kind=kLoop, calls=%fused_computation.3 | loop fusion | flops 8388608 | bytes 25231360 | tf_op jit(solution)/shard_map/convert_element_type | solution.py:21
  97.6 0.0 all-to-all-done.3
  97.6 5.0 all-to-all-start.1
  102.6 0.0 copy-start.1
  102.6 17.6 %copy.25 = f32[16,256,1024]{1,0,2:T(8,128)} copy(f32[16,256,1024]{2,1,0:T(8,128)} %param.5) | data formatting | bytes 33554432 | tf_op args[0]
  120.2 0.0 copy-done.1
  120.2 0.2 copy.24
  120.4 0.0 copy-start
  120.4 9.7 %divide_convert_fusion.1 = bf16[16,256,1024]{1,0,2:T(8,128)(2,1)} fusion(f32[16,256,1024]{1,0,2:T(8,128)} %copy.25, f32[16,1024]{0,1:T(8,128)S(1)} %copy.24), kind=kLoop, calls=%fused_computation.5 | loop fusion | flops 8388608 | bytes 25231360 | tf_op jit(solution)/shard_map/convert_element_type | solution.py:20
  130.1 156.3 %all-to-all-done.1 = bf16[16,256,1024]{1,0,2:T(8,128)(2,1)} async-done(((bf16[16,256,1024]{1,0,2:T(8,128)(2,1)}), bf16[16,256,1024]{1,0,2:T(8,128)(2,1)}, u32[]{:S(2)}, u32[]{:S(2)}) %all-to-all-start.1) | async-done | bytes 8388640 | tf_op jit(solution)/shard_map/all_to_all | solution.py:26
  286.4 4.9 all-to-all-start
  291.4 0.0 copy-done
  291.4 0.2 copy.30
  291.6 16.6 %fusion = bf16[16,1024,256]{2,0,1:T(8,128)(2,1)} fusion(f32[16,1024,256]{2,1,0:T(8,128)} %param.7, f32[16,1024]{0,1:T(8,128)S(1)} %copy.30), kind=kLoop, calls=%fused_computation.1 | loop fusion | flops 8388608 | bytes 25231360 | tf_op jit(solution)/shard_map/convert_element_type | solution.py:22
  308.3 167.0 %all-to-all-done = bf16[16,256,1024]{1,0,2:T(8,128)(2,1)} async-done(((bf16[16,256,1024]{1,0,2:T(8,128)(2,1)}), bf16[16,256,1024]{1,0,2:T(8,128)(2,1)}, u32[]{:S(2)}, u32[]{:S(2)}) %all-to-all-start) | async-done | bytes 8388640 | tf_op jit(solution)/shard_map/all_to_all | solution.py:25
  475.3 5.0 all-to-all-start.2
  480.3 0.6 constant_dynamic-slice_fusion
  480.9 0.6 constant_dynamic-slice_fusion.1
  481.5 0.6 constant_dynamic-slice_fusion.2
  482.1 9.1 %all_gather.3 = bf16[2048,64]{0,1:T(8,128)(2,1)S(1)} all-gather(bf16[2048,16]{0,1:T(8,128)(2,1)S(1)} %bitcast.17), channel_id=1, replica_groups=mesh['bank'=4,'zero'=8] {'bank'}, dimensions={1}, use_global_device_ids=true | all-gather | bytes 327680 | tf_op jit(solution)/shard_map/all_gather | solution.py:42
  491.2 12.3 %copy.29 = bf16[16,8,256,128]{3,2,1,0:T(8,128)(2,1)} copy(bf16[16,8,256,128]{2,0,3,1:T(8,128)(2,1)} %bitcast.4) | data formatting | bytes 16777216 | tf_op jit(solution)/shard_map/all_to_all | solution.py:26
  503.5 12.3 %copy.26 = bf16[16,8,256,128]{3,2,1,0:T(8,128)(2,1)} copy(bf16[16,8,256,128]{2,0,3,1:T(8,128)(2,1)} %bitcast.1) | data formatting | bytes 16777216 | tf_op jit(solution)/shard_map/all_to_all | solution.py:25
  515.8 148.4 %all-to-all-done.2 = bf16[16,1024,256]{2,0,1:T(8,128)(2,1)} async-done(((bf16[16,1024,256]{2,0,1:T(8,128)(2,1)}), bf16[16,1024,256]{2,0,1:T(8,128)(2,1)}, u32[]{:S(2)}, u32[]{:S(2)}) %all-to-all-start.2) | async-done | bytes 8388640 | tf_op jit(solution)/shard_map/all_to_all | solution.py:28
  664.1 11.4 %copy.32 = bf16[16,128,8,256]{3,2,1,0:T(8,128)(2,1)} copy(bf16[16,128,8,256]{3,0,1,2:T(8,128)(2,1)} %bitcast.7) | data formatting | bytes 16777216 | tf_op jit(solution)/shard_map/all_to_all | solution.py:28
  675.5 13.4 %all_to_all.53 = bf16[16,128,2048]{2,1,0:T(8,128)(2,1)} reshape(bf16[16,128,8,256]{3,2,1,0:T(8,128)(2,1)} %copy.32) | data formatting | bytes 16777216 | tf_op jit(solution)/shard_map/all_to_all | solution.py:28
  688.9 0.7 copy.42
  (4 shorter events, 0.1 us)
Async XLA Ops:
  7.2 79.7 %all-reduce.3.cloned.1.call-start = ((), (), s32[]{:S(2)}) async-start(), calls=%async_computation.4 | async-start | bytes 393216 | tf_op jit(solution)/shard_map/psum | solution.py:8
  15.8 12.6 %copy-start.2 = (f32[256,16]{0,1:T(8,128)S(1)}, f32[256,16]{0,1:T(8,128)}, u32[]{:S(2)}) copy-start(f32[256,16]{0,1:T(8,128)} %param.8) | copy-start | bytes 49156
  15.8 12.6 %copy-start.3 = (f32[256]{0:T(256)S(1)}, f32[256]{0:T(256)}, u32[]{:S(2)}) copy-start(f32[256]{0:T(256)} %param.9) | copy-start | bytes 3076
  29.1 68.5 %all-to-all-start.3 = ((bf16[8,256,16]{1,2,0:T(8,128)(2,1)}), bf16[8,256,16]{1,2,0:T(8,128)(2,1)S(1)}, u32[]{:S(2)}, u32[]{:S(2)}) async-start(bf16[8,256,16]{1,2,0:T(8,128)(2,1)} %stack.2), calls=%async_computation.3 | async-start | bytes 131072 | tf_op jit(solution)/shard_map/all_to_all | solution.py:40
  97.6 188.8 %all-to-all-start.1 = ((bf16[16,256,1024]{1,0,2:T(8,128)(2,1)}), bf16[16,256,1024]{1,0,2:T(8,128)(2,1)}, u32[]{:S(2)}, u32[]{:S(2)}) async-start(bf16[16,256,1024]{1,0,2:T(8,128)(2,1)} %divide_convert_fusion), calls=%async_computation.1 | async-start | bytes 16777216 | tf_op jit(solution)/shard_map/all_to_all | solution.py:26
  102.6 17.6 %copy-start.1 = (f32[16,1024]{1,0:T(8,128)S(1)}, f32[16,1024]{1,0:T(8,128)}, u32[]{:S(2)}) copy-start(f32[16,1024]{1,0:T(8,128)} %get-tuple-element.7) | copy-start | bytes 196612
  120.4 171.0 %copy-start = (f32[16,1024]{1,0:T(8,128)S(1)}, f32[16,1024]{1,0:T(8,128)}, u32[]{:S(2)}) copy-start(f32[16,1024]{1,0:T(8,128)} %get-tuple-element.9) | copy-start | bytes 196612
  286.4 188.8 %all-to-all-start = ((bf16[16,256,1024]{1,0,2:T(8,128)(2,1)}), bf16[16,256,1024]{1,0,2:T(8,128)(2,1)}, u32[]{:S(2)}, u32[]{:S(2)}) async-start(bf16[16,256,1024]{1,0,2:T(8,128)(2,1)} %divide_convert_fusion.1), calls=%async_computation | async-start | bytes 16777216 | tf_op jit(solution)/shard_map/all_to_all | solution.py:25
  475.3 188.9 %all-to-all-start.2 = ((bf16[16,1024,256]{2,0,1:T(8,128)(2,1)}), bf16[16,1024,256]{2,0,1:T(8,128)(2,1)}, u32[]{:S(2)}, u32[]{:S(2)}) async-start(bf16[16,1024,256]{2,0,1:T(8,128)(2,1)} %fusion), calls=%async_computation.2 | async-start | bytes 16777216 | tf_op jit(solution)/shard_map/all_to_all | solution.py:28
Sparse Core Ops, SparseCore 0:
  28.6 58.2 all-reduce.2
